TPU v7x, 32 devices: a whole 2x2x4 slice. The times are simulated.
32 devices in a mesh: subj: 2 (over y), row: 4 (over x, core), col: 4 (over z).
Axes of the slice: x: 2, y: 2, z: 4, core: 2. Of those that a mesh axis runs over, the one named last changes fastest.
Arguments:
- series: float32 [800, 4096], P(None, ('subj', 'row', 'col')), parts along dimension 1, as said below
- keep_mask: int32 [32, 16], P(('subj', 'row'), 'col'), parts along dimension 0, may hold values from 0 to 1, as said below
- row_owner: int32 [32], P('subj'), parts along dimension 0, may hold values from 0 to 3, as said below
Outputs:
- owned_tiles: bfloat16 [8, 4, 8, 128, 128], P(('subj', 'row'), 'col'), parts along dimension 0
- owned_ids: int32 [8, 4, 8], P(('subj', 'row'), 'col'), parts along dimension 0
There are 2 independent parts, one for each index of `subj`. A program takes and returns all parts, laid end to end along the dimension named above; each array names one. Nothing has to cross between parts.
Inputs may be any that keep to these rules, and one draw needn't show every extreme that they name: Each voxel's series varies over time. `keep_mask`: of the 4 tiles that one tile row has in one column block, at most 2 are kept; in every draw one owner keeps exactly 2 in each of its tile rows in some column block. `row_owner`: the 4 tile rows of a row block have 4 different owners, and every owner holds 4 tile rows, from 4 different row blocks.
All inputs are finite; a program needn't handle non-finite values.
Results may differ from a plain program's by a relative error of at most 0.0042.
Values may be sent and summed in bfloat16 or wider, within the bound.
A program may use at most 64 MiB of HBM per device.

v0:
```python
import functools

import jax
import jax.numpy as jnp
from jax import lax
from jax.experimental import pallas as pl
from jax.experimental.pallas import tpu as pltpu
from jax.sharding import PartitionSpec as P

TILE = 128
EPSILON = 1e-05
MESH = pl.DeviceIdType.MESH


PIECES = 4


def peers(n_row, r):
    if n_row % 2:
        return [lax.rem(r + k, n_row) for k in range(1, n_row)]
    chips = n_row // 2
    pairs = [(i, j) for i in range(1, chips) for j in range(2)] + [(0, 1)]
    return [
        lax.rem(lax.div(r, 2) + i, chips) * 2 + lax.rem(lax.rem(r, 2) + j, 2) for i, j in pairs
    ]


def kernel(
    n_row,
    n_col,
    series_hbm,
    keep_hbm,
    owner_hbm,
    inbox,
    plan,
    series,
    keep_smem,
    keep_vmem,
    owner_smem,
    row_main,
    row_rest,
    rest_part,
    col_block,
    grid,
    outbox,
    keep_all,
    keep_all_smem,
    load_sem,
    small_sem,
    keep_sem,
    z_send,
    z_recv,
    x_send,
    x_recv,
    t_send,
    t_recv,
    m_send,
    m_recv,
):
    frames = series.shape[0]
    rt, ct = keep_smem.shape
    cap = outbox.shape[1]
    slots = plan.shape[1]
    main = row_main.shape[2]
    rest = frames - main
    step = TILE // PIECES
    order = ([PIECES] if rest else []) + list(range(PIECES))
    r = lax.axis_index("row")
    c = lax.axis_index("col")
    others = peers(n_row, r)
    has_left = c > 0
    has_right = c < n_col - 1

    load = pltpu.make_async_copy(series_hbm, series, load_sem)
    load.start()
    small = [
        pltpu.make_async_copy(keep_hbm, keep_vmem, small_sem.at[0]),
        pltpu.make_async_copy(keep_hbm, keep_smem, small_sem.at[1]),
        pltpu.make_async_copy(owner_hbm, owner_smem, small_sem.at[2]),
    ]
    for copy in small:
        copy.start()

    barrier = pltpu.get_barrier_semaphore()
    for other in others:
        pl.semaphore_signal(barrier, inc=1, device_id={"row": other}, device_id_type=MESH)

    @pl.when(has_left)
    def _():
        pl.semaphore_signal(barrier, inc=1, device_id={"col": c - 1}, device_id_type=MESH)

    @pl.when(has_right)
    def _():
        pl.semaphore_signal(barrier, inc=1, device_id={"col": c + 1}, device_id_type=MESH)

    for copy in small:
        copy.wait()
    load.wait()
    values = series[...]
    average = jnp.sum(values, axis=0, keepdims=True) * (1.0 / frames)
    centred = values - average
    spread = jnp.sum(centred * centred, axis=0, keepdims=True) * (1.0 / frames)
    scale = lax.rsqrt(spread + EPSILON)

    pl.semaphore_wait(
        barrier, n_row - 1 + has_left.astype(jnp.int32) + has_right.astype(jnp.int32)
    )

    def z_copy(shard, chunk, side, target):
        if chunk == PIECES:
            part = row_rest.at[shard]
        else:
            part = row_main.at[shard, pl.ds(chunk * step, step), :]
        return pltpu.make_async_remote_copy(
            src_ref=part,
            dst_ref=part,
            send_sem=z_send.at[side, shard, chunk],
            recv_sem=z_recv.at[shard, chunk],
            device_id={"col": target},
            device_id_type=MESH,
        )

    def to_right(shard, chunk):
        return z_copy(shard, chunk, 0, c + 1)

    def to_left(shard, chunk):
        return z_copy(shard, chunk, 1, c - 1)

    def row_copy(k, src, dst, send, recv):
        return pltpu.make_async_remote_copy(
            src_ref=src,
            dst_ref=dst,
            send_sem=send,
            recv_sem=recv,
            device_id={"row": others[k]},
            device_id_type=MESH,
        )

    def mask_copy(k):
        return row_copy(k, keep_vmem, keep_all.at[r], m_send.at[k], m_recv.at[k])

    def scored_copy(k):
        return row_copy(k, col_block.at[r], col_block.at[r], x_send.at[k], x_recv.at[k])

    def tile_copy(k, v):
        part = pl.ds(v * step, step)
        return row_copy(
            k,
            outbox.at[k, :, part, :],
            inbox.at[pl.ds(r * cap, cap), part, :],
            t_send.at[k, v],
            t_recv.at[k, v],
        )

    peer_range = range(n_row - 1)
    for k in peer_range:
        mask_copy(k).start()
    keep_all[r] = keep_vmem[...]

    scored = centred * scale
    if rest:
        row_rest[c] = scored[main:].astype(jnp.bfloat16)
    flipped = jnp.transpose(scored[:main]).astype(jnp.bfloat16)
    row_main[c] = flipped

    for j in order:

        @pl.when(has_right)
        def _():
            to_right(c, j).start()

        @pl.when(has_left)
        def _():
            to_left(c, j).start()

    col_block[r] = scored.astype(jnp.bfloat16)
    for k in peer_range:
        scored_copy(k).start()

    width = 2 if n_row % 2 == 0 else 1

    def over_columns(body):
        if n_row <= 4:
            for p in range(n_row // width):
                body(p)
        else:

            def step_body(p, carry):
                body(p)
                return carry

            lax.fori_loop(0, n_row // width, step_body, 0)

    def columns(p, part):
        return jnp.concatenate([col_block[p * width + w, part, :] for w in range(width)], axis=1)

    def dot(left, right, axis):
        return lax.dot_general(
            left, right, (((axis,), (0,)), ((), ())), preferred_element_type=jnp.float32
        )

    def multiply_rest(m):
        def body(p):
            rest_part[p] = dot(row_rest[m], columns(p, pl.ds(main, rest)), 0)

        if rest:
            over_columns(body)

    def multiply_rows(m, rows):
        def body(p):
            product = dot(row_main[m, rows, :], columns(p, pl.ds(0, main)), 1)
            if rest:
                product = product + rest_part[p, rows, :]
            product = (product * (1.0 / frames)).astype(jnp.bfloat16)
            for w in range(width):
                grid[m, p * width + w, rows, :] = product[:, w * TILE : (w + 1) * TILE]

        over_columns(body)

    def multiply(m):
        multiply_rest(m)
        multiply_rows(m, pl.ds(0, TILE))

    def pack_plan():
        keep_copy = pltpu.make_async_copy(keep_all, keep_all_smem, keep_sem)
        keep_copy.start()
        keep_copy.wait()
        lanes = lax.broadcasted_iota(jnp.int32, (1, slots), 1)
        ids = jnp.full((1, slots), -1, jnp.int32)
        source = jnp.full((1, slots), n_row * cap, jnp.int32)
        total = jnp.int32(0)
        for b in range(n_row):
            line = jnp.int32(0)
            for i in range(rt):
                line = jnp.where(owner_smem[b * rt + i] == r, i, line)
            start = total
            for j in range(ct):
                kept = keep_all_smem[b, line, j]
                name = (b * rt + line) * (ct * n_col) + c * ct + j
                here = (lanes == total) & (kept == 1)
                ids = jnp.where(here, name, ids)
                source = jnp.where(here, b * cap + total - start, source)
                total = total + kept
        plan[0:1, :] = ids
        plan[1:2, :] = source
        inbox[n_row * cap] = jnp.zeros((TILE, TILE), jnp.bfloat16)

    def choose(target):
        line = jnp.int32(0)
        for i in range(rt):
            line = jnp.where(owner_smem[r * rt + i] == target, i, line)
        picks = [jnp.int32(0)] * cap
        count = jnp.int32(0)
        for j in range(ct):
            kept = keep_smem[line, j]
            for s in range(cap):
                picks[s] = jnp.where((kept == 1) & (count == s), j, picks[s])
            count = count + kept
        return line, picks

    for hop in range(1, n_col - 1):
        for j in order:

            @pl.when(c - hop >= 0)
            def _():
                to_right(c - hop, j).wait_recv()

                @pl.when(has_right)
                def _():
                    to_right(c - hop, j).start()

            @pl.when(c + hop < n_col)
            def _():
                to_left(c + hop, j).wait_recv()

                @pl.when(has_left)
                def _():
                    to_left(c + hop, j).start()

    for k in peer_range:
        mask_copy(k).wait_recv()
    pack_plan()
    choices = [choose(target) for target in others + [r]]
    for k in peer_range:
        scored_copy(k).wait_recv()
    multiply(c)
    for near in range(1, n_col - 1):

        @pl.when(c - near >= 0)
        def _():
            multiply(c - near)

        @pl.when(c + near < n_col)
        def _():
            multiply(c + near)

    last = n_col - 1
    for j in order:
        if last:

            @pl.when(c == last)
            def _():
                to_right(0, j).wait_recv()
                if j == PIECES:
                    multiply_rest(0)
                else:
                    multiply_rows(0, pl.ds(j * step, step))

            @pl.when(c == 0)
            def _():
                to_left(last, j).wait_recv()
                if j == PIECES:
                    multiply_rest(last)
                else:
                    multiply_rows(last, pl.ds(j * step, step))

        if j == PIECES:
            continue
        rows = pl.ds(j * step, step)
        for k in peer_range:
            line, picks = choices[k]
            for s in range(cap):
                outbox[k, s, rows, :] = grid[line, picks[s], rows, :]
            tile_copy(k, j).start()
        line, picks = choices[-1]
        for s in range(cap):
            inbox[r * cap + s, rows, :] = grid[line, picks[s], rows, :]

    for j in order:
        for hop in range(n_col):

            @pl.when((c - hop >= 0) & has_right)
            def _():
                to_right(c - hop, j).wait_send()

            @pl.when((c + hop < n_col) & has_left)
            def _():
                to_left(c + hop, j).wait_send()

    for k in peer_range:
        mask_copy(k).wait_send()
        scored_copy(k).wait_send()
        for v in range(PIECES):
            tile_copy(k, v).wait()


def pack(inbox, plan_smem, plan_vmem, tiles_out, ids_out, sems):
    copies = [
        pltpu.make_async_copy(inbox.at[plan_smem[1, t]], tiles_out.at[t], sems.at[t])
        for t in range(tiles_out.shape[0])
    ]
    for copy in copies:
        copy.start()
    ids_out[...] = plan_vmem[0:1, :]
    for copy in copies:
        copy.wait()


def shards(n_row, n_col, series, keep_mask, row_owner):
    frames = series.shape[0]
    rt, ct = keep_mask.shape
    cap = max(2, 3 * ct // 8)
    slots = rt * cap
    main = frames // TILE * TILE
    rest = max(frames - main, 16)
    links = max(n_row - 1, 1)
    width = 2 if n_row % 2 == 0 else 1
    dma = pltpu.SemaphoreType.DMA
    vmem = pl.BlockSpec(memory_space=pltpu.VMEM)
    hbm = pl.BlockSpec(memory_space=pltpu.HBM)
    inbox, plan = pl.pallas_call(
        functools.partial(kernel, n_row, n_col),
        out_shape=(
            jax.ShapeDtypeStruct((n_row * cap + 1, TILE, TILE), jnp.bfloat16),
            jax.ShapeDtypeStruct((2, slots), jnp.int32),
        ),
        in_specs=[hbm, hbm, hbm],
        out_specs=(vmem, vmem),
        scratch_shapes=[
            pltpu.VMEM((frames, TILE), jnp.float32),
            pltpu.SMEM((rt, ct), jnp.int32),
            pltpu.VMEM((rt, ct), jnp.int32),
            pltpu.SMEM(row_owner.shape, jnp.int32),
            pltpu.VMEM((n_col, TILE, main), jnp.bfloat16),
            pltpu.VMEM((n_col, rest, TILE), jnp.bfloat16),
            pltpu.VMEM((n_row // width, TILE, width * TILE), jnp.float32),
            pltpu.VMEM((n_row, frames, TILE), jnp.bfloat16),
            pltpu.VMEM((rt, ct, TILE, TILE), jnp.bfloat16),
            pltpu.VMEM((links, cap, TILE, TILE), jnp.bfloat16),
            pltpu.VMEM((n_row, rt, ct), jnp.int32),
            pltpu.SMEM((n_row, rt, ct), jnp.int32),
            dma(()),
            dma((3,)),
            dma(()),
            dma((2, n_col, PIECES + 1)),
            dma((n_col, PIECES + 1)),
            dma((links,)),
            dma((links,)),
            dma((links, PIECES)),
            dma((links, PIECES)),
            dma((links,)),
            dma((links,)),
        ],
        compiler_params=pltpu.CompilerParams(
            collective_id=0, has_side_effects=True, vmem_limit_bytes=32 * 1024 * 1024
        ),
    )(*(pltpu.with_memory_space_constraint(x, pltpu.HBM) for x in (series, keep_mask, row_owner)))
    tiles, ids = pl.pallas_call(
        pack,
        out_shape=(
            jax.ShapeDtypeStruct((slots, TILE, TILE), jnp.bfloat16),
            jax.ShapeDtypeStruct((1, slots), jnp.int32),
        ),
        in_specs=[vmem, pl.BlockSpec(memory_space=pltpu.SMEM), vmem],
        out_specs=(hbm, vmem),
        scratch_shapes=[dma((slots,))],
        compiler_params=pltpu.CompilerParams(vmem_limit_bytes=16 * 1024 * 1024),
    )(inbox, plan, plan)
    return tiles.reshape(1, 1, slots, TILE, TILE), ids.reshape(1, 1, slots)


def solution(mesh):
    in_specs = (P(None, ("subj", "row", "col")), P(("subj", "row"), "col"), P("subj"))
    out_specs = (P(("subj", "row"), "col", None, None, None), P(("subj", "row"), "col", None))
    return jax.shard_map(
        functools.partial(shards, mesh.shape["row"], mesh.shape["col"]),
        mesh=mesh,
        in_specs=in_specs,
        out_specs=out_specs,
        check_vma=False,
    )
```

profile of v0, /device:TPU:0, one launch (start us, length us, event | category | flops | bytes accessed | tf_op | source)
XLA Modules:
  0.0 25.3 jit_solution(14595319140248373054)
XLA Ops:
  0.6 22.8 %shard_map.50 = (bf16[9,128,128]{2,1,0:T(8,128)(2,1)S(1)}, s32[2,8]{1,0:T(2,128)S(1)}) custom-call(f32[800,128]{1,0:T(8,128)} %series_hbm.1, s32[4,4]{1,0:T(4,128)} %keep_hbm.1, s32[16]{0:T(128)} %owner_hbm.1), custom_call_target="tpu_custom_call" | custom-call | tf_op jit(solution)/shard_map/pallas_call | solution.py:371
  23.4 1.8 %shard_map.51 = (bf16[8,128,128]{2,1,0:T(8,128)(2,1)}, s32[1,8]{1,0:T(1,128)}) custom-call(bf16[9,128,128]{2,1,0:T(8,128)(2,1)S(1)} %get-tuple-element.6.inbox, s32[2,8]{1,0:T(2,128)S(1)} %get-tuple-element.7.plan_smem.plan_vmem, s32[2,8]{1,0:T(2,128)S(1)} %get-tuple-element.7.plan_smem.plan_vmem), custom_call_target="tpu_custom_call" | custom-call | tf_op jit(solution)/shard_map/pallas_call | solution.py:408
where the time goes:
time: 25.4 us; the launch traced here: 25.3 us
  Pallas kernels  24.6 us (97%)
  between operations  0.64 us (3%)
    pallas_call x1, Pallas kernels, shards(): pl.pallas_call(functools.partial(kernel, n_row, n_col), out_shape=(jax.Sh...  22.8 us
    pallas_call x1, Pallas kernels, shards(): pl.pallas_call(pack, out_shape=(jax.ShapeDtypeStruct((slots, TILE, TILE),...  1.82 us

commit v1 on v0

--- a/solution.py
+++ b/solution.py
@@ -31,8 +31,8 @@
     series_hbm,
     keep_hbm,
     owner_hbm,
-    inbox,
-    plan,
+    packed,
+    ids_out,
     series,
     keep_smem,
     keep_vmem,
@@ -43,6 +43,8 @@
     col_block,
     grid,
     outbox,
+    inbox,
+    plan,
     keep_all,
     keep_all_smem,
     load_sem,
@@ -60,7 +62,7 @@
     frames = series.shape[0]
     rt, ct = keep_smem.shape
     cap = outbox.shape[1]
-    slots = plan.shape[1]
+    slots = packed.shape[0]
     main = row_main.shape[2]
     rest = frames - main
     step = TILE // PIECES
@@ -227,22 +229,24 @@
         keep_copy.wait()
         lanes = lax.broadcasted_iota(jnp.int32, (1, slots), 1)
         ids = jnp.full((1, slots), -1, jnp.int32)
-        source = jnp.full((1, slots), n_row * cap, jnp.int32)
         total = jnp.int32(0)
+        starts = []
         for b in range(n_row):
             line = jnp.int32(0)
             for i in range(rt):
                 line = jnp.where(owner_smem[b * rt + i] == r, i, line)
-            start = total
+            starts.append(total)
             for j in range(ct):
                 kept = keep_all_smem[b, line, j]
                 name = (b * rt + line) * (ct * n_col) + c * ct + j
-                here = (lanes == total) & (kept == 1)
-                ids = jnp.where(here, name, ids)
-                source = jnp.where(here, b * cap + total - start, source)
+                ids = jnp.where((lanes == total) & (kept == 1), name, ids)
                 total = total + kept
-        plan[0:1, :] = ids
-        plan[1:2, :] = source
+        ids_out[...] = ids
+        for s in range(slots):
+            source = jnp.int32(s)
+            for b in range(1, n_row):
+                source = jnp.where(s >= starts[b], b * cap + s - starts[b], source)
+            plan[s] = jnp.where(s < total, source, n_row * cap)
         inbox[n_row * cap] = jnp.zeros((TILE, TILE), jnp.bfloat16)
 
     def choose(target):
@@ -343,15 +347,25 @@
         for v in range(PIECES):
             tile_copy(k, v).wait()
 
-
-def pack(inbox, plan_smem, plan_vmem, tiles_out, ids_out, sems):
+    if slots <= 8:
+        for s in range(slots):
+            packed[s] = inbox[plan[s]]
+    else:
+
+        def pack_slot(s, carry):
+            packed[s] = inbox[plan[s]]
+            return carry
+
+        lax.fori_loop(0, slots, pack_slot, 0)
+
+
+def write(tiles, ids, tiles_out, ids_out, sems):
     copies = [
-        pltpu.make_async_copy(inbox.at[plan_smem[1, t]], tiles_out.at[t], sems.at[t])
-        for t in range(tiles_out.shape[0])
+        pltpu.make_async_copy(tiles, tiles_out, sems.at[0]),
+        pltpu.make_async_copy(ids, ids_out, sems.at[1]),
     ]
     for copy in copies:
         copy.start()
-    ids_out[...] = plan_vmem[0:1, :]
     for copy in copies:
         copy.wait()
 
@@ -368,11 +382,11 @@
     dma = pltpu.SemaphoreType.DMA
     vmem = pl.BlockSpec(memory_space=pltpu.VMEM)
     hbm = pl.BlockSpec(memory_space=pltpu.HBM)
-    inbox, plan = pl.pallas_call(
+    packed, ids = pl.pallas_call(
         functools.partial(kernel, n_row, n_col),
         out_shape=(
-            jax.ShapeDtypeStruct((n_row * cap + 1, TILE, TILE), jnp.bfloat16),
-            jax.ShapeDtypeStruct((2, slots), jnp.int32),
+            jax.ShapeDtypeStruct((slots, TILE, TILE), jnp.bfloat16),
+            jax.ShapeDtypeStruct((1, slots), jnp.int32),
         ),
         in_specs=[hbm, hbm, hbm],
         out_specs=(vmem, vmem),
@@ -387,6 +401,8 @@
             pltpu.VMEM((n_row, frames, TILE), jnp.bfloat16),
             pltpu.VMEM((rt, ct, TILE, TILE), jnp.bfloat16),
             pltpu.VMEM((links, cap, TILE, TILE), jnp.bfloat16),
+            pltpu.VMEM((n_row * cap + 1, TILE, TILE), jnp.bfloat16),
+            pltpu.SMEM((slots,), jnp.int32),
             pltpu.VMEM((n_row, rt, ct), jnp.int32),
             pltpu.SMEM((n_row, rt, ct), jnp.int32),
             dma(()),
@@ -406,16 +422,16 @@
         ),
     )(*(pltpu.with_memory_space_constraint(x, pltpu.HBM) for x in (series, keep_mask, row_owner)))
     tiles, ids = pl.pallas_call(
-        pack,
+        write,
         out_shape=(
             jax.ShapeDtypeStruct((slots, TILE, TILE), jnp.bfloat16),
             jax.ShapeDtypeStruct((1, slots), jnp.int32),
         ),
-        in_specs=[vmem, pl.BlockSpec(memory_space=pltpu.SMEM), vmem],
-        out_specs=(hbm, vmem),
-        scratch_shapes=[dma((slots,))],
+        in_specs=[vmem, vmem],
+        out_specs=(hbm, hbm),
+        scratch_shapes=[dma((2,))],
         compiler_params=pltpu.CompilerParams(vmem_limit_bytes=16 * 1024 * 1024),
-    )(inbox, plan, plan)
+    )(packed, ids)
     return tiles.reshape(1, 1, slots, TILE, TILE), ids.reshape(1, 1, slots)
 
 

time: 25.4 us -> 24.3 us (0.957)
  Pallas kernels: 24.6 us -> 23.5 us
    pallas_call x1, Pallas kernels: 1.82 us -> 0.72 us  [shards(): pl.pallas_call(write, out_shape=(jax.ShapeDtypeStruct((slots, TILE, TILE)...]
where the time goes in v1:
time: 24.3 us; the launch traced here: 24.2 us
  Pallas kernels  23.5 us (97%)
  between operations  0.64 us (3%)
    pallas_call x1, Pallas kernels, shards(): pl.pallas_call(functools.partial(kernel, n_row, n_col), out_shape=(jax.Sh...  22.8 us
    pallas_call x1, Pallas kernels, shards(): pl.pallas_call(write, out_shape=(jax.ShapeDtypeStruct((slots, TILE, TILE)...  0.72 us

profile of v1, /device:TPU:0, one launch (start us, length us, event | category | flops | bytes accessed | tf_op | source)
XLA Modules:
  0.0 24.2 jit_solution(9062079547758117202)
XLA Ops:
  0.6 22.8 %shard_map.50 = (bf16[8,128,128]{2,1,0:T(8,128)(2,1)S(1)}, s32[1,8]{1,0:T(1,128)S(1)}) custom-call(f32[800,128]{1,0:T(8,128)} %series_hbm.1, s32[4,4]{1,0:T(4,128)} %keep_hbm.1, s32[16]{0:T(128)} %owner_hbm.1), custom_call_target="tpu_custom_call" | custom-call | tf_op jit(solution)/shard_map/pallas_call | solution.py:385
  23.5 0.7 %shard_map.51 = (bf16[8,128,128]{2,1,0:T(8,128)(2,1)}, s32[1,8]{1,0:T(1,128)}) custom-call(bf16[8,128,128]{2,1,0:T(8,128)(2,1)S(1)} %get-tuple-element.6.tiles, s32[1,8]{1,0:T(1,128)S(1)} %get-tuple-element.7.ids), custom_call_target="tpu_custom_call" | custom-call | tf_op jit(solution)/shard_map/pallas_call | solution.py:424

commit v2 on v1

--- a/solution.py
+++ b/solution.py
@@ -12,7 +12,10 @@
 MESH = pl.DeviceIdType.MESH
 
 
-PIECES = 4
+LOADS = 8
+SIZES = (64, 32, 32)
+PIECES = len(SIZES)
+PARTS = [pl.ds(sum(SIZES[:i]), size) for i, size in enumerate(SIZES)]
 
 
 def peers(n_row, r):
@@ -47,6 +50,7 @@
     plan,
     keep_all,
     keep_all_smem,
+    right_sem,
     load_sem,
     small_sem,
     keep_sem,
@@ -65,7 +69,6 @@
     slots = packed.shape[0]
     main = row_main.shape[2]
     rest = frames - main
-    step = TILE // PIECES
     order = ([PIECES] if rest else []) + list(range(PIECES))
     r = lax.axis_index("row")
     c = lax.axis_index("col")
@@ -73,8 +76,17 @@
     has_left = c > 0
     has_right = c < n_col - 1
 
-    load = pltpu.make_async_copy(series_hbm, series, load_sem)
-    load.start()
+    cuts = [frames * i // LOADS // 8 * 8 for i in range(LOADS)] + [frames]
+    loads = [
+        pltpu.make_async_copy(
+            series_hbm.at[pl.ds(low, high - low), :],
+            series.at[pl.ds(low, high - low), :],
+            load_sem.at[i],
+        )
+        for i, (low, high) in enumerate(zip(cuts[:-1], cuts[1:]))
+    ]
+    for load in loads:
+        load.start()
     small = [
         pltpu.make_async_copy(keep_hbm, keep_vmem, small_sem.at[0]),
         pltpu.make_async_copy(keep_hbm, keep_smem, small_sem.at[1]),
@@ -87,32 +99,33 @@
     for other in others:
         pl.semaphore_signal(barrier, inc=1, device_id={"row": other}, device_id_type=MESH)
 
-    @pl.when(has_left)
-    def _():
-        pl.semaphore_signal(barrier, inc=1, device_id={"col": c - 1}, device_id_type=MESH)
-
     @pl.when(has_right)
     def _():
         pl.semaphore_signal(barrier, inc=1, device_id={"col": c + 1}, device_id_type=MESH)
 
     for copy in small:
         copy.wait()
-    load.wait()
+    total = jnp.zeros((8, TILE), jnp.float32)
+    for load, low, high in zip(loads, cuts[:-1], cuts[1:]):
+        load.wait()
+        total = total + jnp.sum(series[low:high, :].reshape(-1, 8, TILE), axis=0)
+    average = jnp.sum(total, axis=0, keepdims=True) * (1.0 / frames)
     values = series[...]
-    average = jnp.sum(values, axis=0, keepdims=True) * (1.0 / frames)
     centred = values - average
     spread = jnp.sum(centred * centred, axis=0, keepdims=True) * (1.0 / frames)
     scale = lax.rsqrt(spread + EPSILON)
 
-    pl.semaphore_wait(
-        barrier, n_row - 1 + has_left.astype(jnp.int32) + has_right.astype(jnp.int32)
-    )
+    pl.semaphore_wait(barrier, n_row - 1 + has_left.astype(jnp.int32))
+
+    @pl.when(has_left)
+    def _():
+        pl.semaphore_signal(right_sem, inc=1, device_id={"col": c - 1}, device_id_type=MESH)
 
     def z_copy(shard, chunk, side, target):
         if chunk == PIECES:
             part = row_rest.at[shard]
         else:
-            part = row_main.at[shard, pl.ds(chunk * step, step), :]
+            part = row_main.at[shard, PARTS[chunk], :]
         return pltpu.make_async_remote_copy(
             src_ref=part,
             dst_ref=part,
@@ -145,7 +158,7 @@
         return row_copy(k, col_block.at[r], col_block.at[r], x_send.at[k], x_recv.at[k])
 
     def tile_copy(k, v):
-        part = pl.ds(v * step, step)
+        part = PARTS[v]
         return row_copy(
             k,
             outbox.at[k, :, part, :],
@@ -167,10 +180,6 @@
 
     for j in order:
 
-        @pl.when(has_right)
-        def _():
-            to_right(c, j).start()
-
         @pl.when(has_left)
         def _():
             to_left(c, j).start()
@@ -178,6 +187,12 @@
     col_block[r] = scored.astype(jnp.bfloat16)
     for k in peer_range:
         scored_copy(k).start()
+
+    @pl.when(has_right)
+    def _():
+        pl.semaphore_wait(right_sem, 1)
+        for j in order:
+            to_right(c, j).start()
 
     width = 2 if n_row % 2 == 0 else 1
 
@@ -265,6 +280,14 @@
     for hop in range(1, n_col - 1):
         for j in order:
 
+            @pl.when(c + hop < n_col)
+            def _():
+                to_left(c + hop, j).wait_recv()
+
+                @pl.when(has_left)
+                def _():
+                    to_left(c + hop, j).start()
+
             @pl.when(c - hop >= 0)
             def _():
                 to_right(c - hop, j).wait_recv()
@@ -272,14 +295,6 @@
                 @pl.when(has_right)
                 def _():
                     to_right(c - hop, j).start()
-
-            @pl.when(c + hop < n_col)
-            def _():
-                to_left(c + hop, j).wait_recv()
-
-                @pl.when(has_left)
-                def _():
-                    to_left(c + hop, j).start()
 
     for k in peer_range:
         mask_copy(k).wait_recv()
@@ -308,7 +323,7 @@
                 if j == PIECES:
                     multiply_rest(0)
                 else:
-                    multiply_rows(0, pl.ds(j * step, step))
+                    multiply_rows(0, PARTS[j])
 
             @pl.when(c == 0)
             def _():
@@ -316,11 +331,11 @@
                 if j == PIECES:
                     multiply_rest(last)
                 else:
-                    multiply_rows(last, pl.ds(j * step, step))
+                    multiply_rows(last, PARTS[j])
 
         if j == PIECES:
             continue
-        rows = pl.ds(j * step, step)
+        rows = PARTS[j]
         for k in peer_range:
             line, picks = choices[k]
             for s in range(cap):
@@ -405,7 +420,8 @@
             pltpu.SMEM((slots,), jnp.int32),
             pltpu.VMEM((n_row, rt, ct), jnp.int32),
             pltpu.SMEM((n_row, rt, ct), jnp.int32),
-            dma(()),
+            pltpu.SemaphoreType.REGULAR,
+            dma((LOADS,)),
             dma((3,)),
             dma(()),
             dma((2, n_col, PIECES + 1)),

time: 24.3 us -> 24.1 us (level)
    pallas_call x1, Pallas kernels: 22.8 us -> 22.5 us  [shards(): pl.pallas_call(functools.partial(kernel, n_row, n_col), out_shape=(jax.Sh...]
where the time goes in v2:
time: 24.1 us; the launch traced here: 23.9 us
  Pallas kernels  23.3 us (97%)
  between operations  0.64 us (3%)
    pallas_call x1, Pallas kernels, shards(): pl.pallas_call(functools.partial(kernel, n_row, n_col), out_shape=(jax.Sh...  22.5 us
    pallas_call x1, Pallas kernels, shards(): pl.pallas_call(write, out_shape=(jax.ShapeDtypeStruct((slots, TILE, TILE)...  0.72 us

profile of v2, /device:TPU:0, one launch (start us, length us, event | category | flops | bytes accessed | tf_op | source)
XLA Modules:
  0.0 23.9 jit_solution(3268049983791188216)
XLA Ops:
  0.6 22.5 %shard_map.50 = (bf16[8,128,128]{2,1,0:T(8,128)(2,1)S(1)}, s32[1,8]{1,0:T(1,128)S(1)}) custom-call(f32[800,128]{1,0:T(8,128)} %series_hbm.1, s32[4,4]{1,0:T(4,128)} %keep_hbm.1, s32[16]{0:T(128)} %owner_hbm.1), custom_call_target="tpu_custom_call" | custom-call | tf_op jit(solution)/shard_map/pallas_call | solution.py:400
  23.2 0.7 %shard_map.51 = (bf16[8,128,128]{2,1,0:T(8,128)(2,1)}, s32[1,8]{1,0:T(1,128)}) custom-call(bf16[8,128,128]{2,1,0:T(8,128)(2,1)S(1)} %get-tuple-element.6.tiles, s32[1,8]{1,0:T(1,128)S(1)} %get-tuple-element.7.ids), custom_call_target="tpu_custom_call" | custom-call | tf_op jit(solution)/shard_map/pallas_call | solution.py:440
